TPU v7x, 128 devices: a whole 4x4x4 slice. The times are simulated.
128 devices in a mesh: member: 1, lon: 2 (over core), lat: 64 (over z, y, x).
Axes of the slice: x: 4, y: 4, z: 4, core: 2. Of those that a mesh axis runs over, the one named last changes fastest.
Arguments:
- field_in: float32 [1, 128, 384, 768], P('member', None, 'lat', 'lon')
- fwd_table: float32 [256, 256, 384], replicated
- inv_table: float32 [256, 256, 384], replicated
- mix_weights: float32 [256, 128, 128, 2], replicated
Outputs:
- output: float32 [1, 128, 384, 768], P('member', None, 'lat', 'lon')
All inputs are finite; a program needn't handle non-finite values.
Results may differ from a plain program's by a relative error of at most 0.00425.
Values are sent between devices in bfloat16 or wider.
A program may use at most 1 GiB of HBM per device.

v0:
```python
import functools
import math
import jax
import jax.numpy as jnp
import numpy as np
from jax import lax
from jax.experimental import pallas as pl
from jax.experimental.pallas import tpu as pltpu
from jax.sharding import PartitionSpec as P

MESH = pl.DeviceIdType.MESH
BF = jnp.bfloat16
F32 = jnp.float32
CH = 128
DEV = 128
CHIPS = 64
TT = 3
JH = 384
DEG = 256
LAT = 384
WCH = 8
WSLOTS = 16
EARLY = 3
BLOCKS = DEG // WCH
GROUP = 64


def chip_order():
    hops = lambda o: sum(min(v, 4 - v) for v in o)
    offsets = [(a, b, c) for a in range(4) for b in range(4) for c in range(4) if a or b or c]
    return sorted(offsets, key=lambda o: (-hops(o), o[2], o[0], o[1]))


ORDER = chip_order()


def pair_of_device():
    q = np.arange(CHIPS)
    colour = (q // 16 + q // 4 % 4 + q % 4) % 2
    chip_pair = colour * (CHIPS // 2) + q // 2
    return (2 * chip_pair[:, None] + np.arange(2)[None, :]).reshape(DEV)


def dft_tables():
    lon_points, waves = 2 * JH, DEG
    phase = np.float32(2.0 * math.pi / lon_points) * (
        (np.arange(waves)[:, None] * np.arange(lon_points)[None, :]) % lon_points).astype(np.float32)
    cos_val, sin_val = np.cos(phase), np.sin(phase)
    k = np.where(np.arange(waves) == 0, 1.0, 2.0).astype(np.float32)[:, None]
    fwd = np.stack([cos_val, -sin_val], axis=1).reshape(2 * waves, lon_points)
    inv = np.stack([k * cos_val, -k * sin_val], axis=1).reshape(2 * waves, lon_points)
    rows = (4 * pair_of_device()[:, None] + np.arange(4)[None, :]).reshape(2 * waves)
    return fwd[rows].astype(BF), inv[rows].astype(BF)


def dot(a, b, ca, cb):
    return lax.dot_general(a, b, (((ca,), (cb,)), ((), ())), preferred_element_type=F32)


def kernel(x_hbm, fwd_hbm, inv_hbm, mix_hbm, dftf_hbm, dfti_hbm, y_ref,
           xv, xb, xr, dftf, dfti, acc, sbuf, rbuf, tabf, tabi, tf, ti, wbuf, wt, gat, xm,
           zf, bf, bfull, sbuf2, rbuf2, rbt, ysend, lsem, wsem, xsem, a1sem, a2sem, yesem):
    h = lax.axis_index("lon")
    p = lax.axis_index("lat")
    d = p * 2 + h
    mate = (0, 1 - h, p)

    def wrap(v):
        return jnp.where(v >= 4, v - 4, v)
    z, y, x = lax.div(p, 16), lax.rem(lax.div(p, 4), 4), lax.rem(p, 4)
    zq = [wrap(z + i) * 16 for i in range(4)]
    yq = [wrap(y + i) * 4 for i in range(4)]
    xq = [wrap(x + i) for i in range(4)]

    pair = 2 * (lax.rem(z + y + x, 2) * (CHIPS // 2) + lax.div(p, 2)) + h

    loads = [
        pltpu.make_async_copy(x_hbm, xv, lsem.at[0]),
        pltpu.make_async_copy(dftf_hbm, dftf, lsem.at[1]),
        pltpu.make_async_copy(fwd_hbm.at[pl.ds(2 * pair, 2)], tabf, lsem.at[2]),
        pltpu.make_async_copy(inv_hbm.at[pl.ds(2 * pair, 2)], tabi, lsem.at[3]),
        pltpu.make_async_copy(dfti_hbm, dfti, lsem.at[4]),
    ]
    loads[0].start()

    barrier = pltpu.get_barrier_semaphore()
    for a, b, c in ORDER:
        for e in range(2):
            pl.semaphore_signal(barrier, inc=1, device_id=(0, e, zq[a] + yq[b] + xq[c]), device_id_type=MESH)
    pl.semaphore_signal(barrier, inc=1, device_id=mate, device_id_type=MESH)
    for c in loads[1:]:
        c.start()

    def wcopy(i, slot):
        return pltpu.make_async_copy(mix_hbm.at[pl.ds(i * WCH, WCH)], wbuf.at[slot], wsem.at[slot])

    loads[0].wait()
    for u in range(2):
        for t in range(TT):
            xb[u, pl.ds(t * CH, CH), :] = xv[u * TT + t].astype(BF)
    for i in range(WSLOTS):
        wcopy(i, i).start()
    loads[1].wait()
    own = pl.ds(pl.multiple_of(h * JH, JH), JH)
    oth = pl.ds(pl.multiple_of((1 - h) * JH, JH), JH)
    acc[...] = dot(dftf[:, own], xb[h], 1, 1)

    krow = lax.broadcasted_iota(jnp.int32, (LAT, LAT), 0)
    tcol = lax.broadcasted_iota(jnp.int32, (LAT, LAT), 1)
    perm = jnp.where(tcol == TT * (krow % DEV) + krow // DEV, 1.0, 0.0).astype(BF)
    loads[2].wait()
    loads[3].wait()
    for m in range(2):
        tf[m] = dot(tabf[m].astype(BF), perm, 1, 1).astype(BF)
        ti[m] = dot(perm, tabi[m].astype(BF), 1, 1).astype(BF)

    def prepare(i, refill):
        slot = lax.rem(i, WSLOTS)
        wcopy(i, slot).wait()

        def prep(l, _):
            for q in range(2):
                w = wbuf[slot, l, pl.ds(q, CH, stride=2), :]
                wt[i * WCH + l, :, q * CH:(q + 1) * CH] = w.astype(BF).T
            return 0
        lax.fori_loop(0, WCH, prep, 0, unroll=True)
        if refill:
            wcopy(i + WSLOTS, slot).start()

    def prepare_blocks(lo, hi, refill):
        def one(i, _):
            prepare(i, refill)
            return 0
        lax.fori_loop(lo, hi, one, 0)

    prepare_blocks(0, EARLY, True)
    bf[...] = jnp.zeros_like(bf)
    pl.semaphore_wait(barrier, DEV - 1)
    xcopy = [pltpu.make_async_remote_copy(xb.at[1 - h, pl.ds(t * CH, CH)], xr.at[pl.ds(t * CH, CH)], xsem.at[t], xsem.at[TT + t],
                                          device_id=mate, device_id_type=MESH) for t in range(TT)]
    for c in xcopy:
        c.start()
    for t in range(TT):
        xcopy[t].wait_recv()
    sbuf[...] = (acc[...] + dot(dftf[:, oth], xr[...], 1, 1)).astype(BF).reshape(DEV, 4, TT * CH)

    def exchange(src, dst, sem):
        for a, b, c in ORDER:
            q = zq[a] + yq[b] + xq[c]
            for e in range(2):
                pltpu.make_async_remote_copy(src.at[2 * q + e], dst.at[d], sem.at[0], sem.at[1],
                                             device_id=(0, e, q), device_id_type=MESH).start()
        pltpu.make_async_remote_copy(src.at[d + 1 - 2 * h], dst.at[d], sem.at[0], sem.at[1],
                                     device_id=mate, device_id_type=MESH).start()
        dst[d] = src[d]
        return pltpu.make_async_remote_copy(src.at[pl.ds(0, DEV - 1)], dst.at[pl.ds(0, DEV - 1)], sem.at[0], sem.at[1],
                                            device_id=mate, device_id_type=MESH)

    first = exchange(sbuf, rbuf, a1sem)

    prepare_blocks(EARLY, BLOCKS - WSLOTS, True)
    prepare_blocks(BLOCKS - WSLOTS, BLOCKS, False)

    first.wait_recv()

    for t in range(TT):
        gat[t] = rbuf[:, :, t * CH:(t + 1) * CH].astype(F32).reshape(4 * DEV, CH)
    for m in range(2):
        for r in range(2):
            for t in range(TT):
                xm[m, t * DEV:(t + 1) * DEV, r * CH:(r + 1) * CH] = gat[t, pl.ds(2 * m + r, DEV, stride=4), :].astype(BF)
    for m in range(2):
        coef = dot(tf[m], xm[m], 1, 0)
        for r in range(2):
            zf[pl.ds(2 * r + m, DEG, stride=4), :] = coef[:, r * CH:(r + 1) * CH]

    row = lax.broadcasted_iota(jnp.int32, (8, CH), 0)
    real = lax.rem(row, 4) < 2
    sign = jnp.where(real, -1.0, 1.0)
    low = lax.broadcasted_iota(jnp.int32, (8, 2 * CH), 0) < 4

    def mix(group, _):
        for u in range(GROUP):
            l = group * GROUP + u
            rows = pl.ds(pl.multiple_of(8 * l, 8), 8)
            coef = zf[rows, :].astype(BF)
            v = jnp.where(low, dot(coef, wt[2 * l], 1, 0), dot(coef, wt[2 * l + 1], 1, 0))
            im = v[:, CH:]
            bf[rows, :] = v[:, :CH] + sign * jnp.where(real, pltpu.roll(im, 6, 0), pltpu.roll(im, 2, 0))
        return 0
    lax.fori_loop(lax.div(pair, GROUP), DEG // 2 // GROUP, mix, 0)

    for m in range(2):
        for r in range(2):
            bfull[m, :, r * CH:(r + 1) * CH] = bf[pl.ds(2 * r + m, DEG, stride=4), :].astype(BF)

    for m in range(2):
        g = dot(ti[m], bfull[m], 1, 0)
        for r in range(2):
            for t in range(TT):
                gat[t, pl.ds(2 * m + r, DEV, stride=4), :] = g[t * DEV:(t + 1) * DEV, r * CH:(r + 1) * CH]

    for t in range(TT):
        sbuf2[:, :, t * CH:(t + 1) * CH] = gat[t].astype(BF).reshape(DEV, 4, CH)
    second = exchange(sbuf2, rbuf2, a2sem)
    loads[4].wait()
    second.wait_recv()

    rbt[...] = rbuf2[...].reshape(2 * DEG, TT * CH).T

    ysend[...] = dot(rbt[...], dfti[:, oth], 1, 0).astype(BF).reshape(TT, CH, JH)
    ycopy = [pltpu.make_async_remote_copy(ysend.at[t], y_ref.at[h * TT + t], yesem.at[t], yesem.at[TT + t],
                                          device_id=mate, device_id_type=MESH) for t in range(TT)]
    for c in ycopy:
        c.start()
    first.wait_send()
    y_ref[pl.ds(h * TT, TT)] = dot(rbt[...], dfti[:, own], 1, 0).astype(BF).reshape(TT, CH, JH)
    for c in ycopy:
        c.wait_recv()

    for c in xcopy + ycopy:
        c.wait_send()
    second.wait_send()


def solution(mesh):
    grid_spec = P('member', None, 'lat', 'lon')
    fwd_np, inv_np = dft_tables()

    def local_layer(field_in, fwd_table, inv_table, mix_weights):
        x = jnp.transpose(field_in[0], (1, 0, 2))
        mix = jnp.transpose(mix_weights, (0, 1, 3, 2)).reshape(DEG, 2 * CH, CH)
        hbm = pl.BlockSpec(memory_space=pltpu.HBM)
        dma2, dma6 = pltpu.SemaphoreType.DMA((2,)), pltpu.SemaphoreType.DMA((2 * TT,))
        y = pl.pallas_call(
            kernel,
            out_shape=jax.ShapeDtypeStruct((2 * TT, CH, JH), BF),
            in_specs=[hbm] * 6,
            out_specs=pl.BlockSpec(memory_space=pltpu.VMEM),
            scratch_shapes=[
                pltpu.VMEM((2 * TT, CH, JH), F32),
                pltpu.VMEM((2, TT * CH, JH), BF),
                pltpu.VMEM((TT * CH, JH), BF),
                pltpu.VMEM((2 * DEG, 2 * JH), BF),
                pltpu.VMEM((2 * DEG, 2 * JH), BF),
                pltpu.VMEM((2 * DEG, TT * CH), F32),
                pltpu.VMEM((DEV, 4, TT * CH), BF),
                pltpu.VMEM((DEV, 4, TT * CH), BF),
                pltpu.VMEM((2, DEG, LAT), F32),
                pltpu.VMEM((2, DEG, LAT), F32),
                pltpu.VMEM((2, DEG, LAT), BF),
                pltpu.VMEM((2, LAT, DEG), BF),
                pltpu.VMEM((WSLOTS, WCH, 2 * CH, CH), F32),
                pltpu.VMEM((DEG, CH, 2 * CH), BF),
                pltpu.VMEM((TT, 4 * DEV, CH), F32),
                pltpu.VMEM((2, LAT, 2 * CH), BF),
                pltpu.VMEM((4 * DEG, CH), F32),
                pltpu.VMEM((4 * DEG, CH), F32),
                pltpu.VMEM((2, DEG, 2 * CH), BF),
                pltpu.VMEM((DEV, 4, TT * CH), BF),
                pltpu.VMEM((DEV, 4, TT * CH), BF),
                pltpu.VMEM((TT * CH, 2 * DEG), BF),
                pltpu.VMEM((TT, CH, JH), BF),
                pltpu.SemaphoreType.DMA((5,)),
                pltpu.SemaphoreType.DMA((WSLOTS,)),
                dma6, dma2, dma2, dma6,
            ],
            compiler_params=pltpu.CompilerParams(collective_id=0, has_side_effects=True, vmem_limit_bytes=48 * 1024 * 1024),
            name="spectral_layer",
        )(*[pltpu.with_memory_space_constraint(v, pltpu.HBM) for v in (x, fwd_table, inv_table, mix, jnp.asarray(fwd_np), jnp.asarray(inv_np))])
        wave = jnp.transpose(y, (1, 0, 2))[None]
        return field_in + jax.nn.gelu(wave.astype(F32), approximate=True)

    return jax.shard_map(local_layer, mesh=mesh, in_specs=(grid_spec, P(), P(), P()), out_specs=grid_spec, check_vma=False)
```

profile of v0, /device:TPU:1, one launch (start us, length us, event | category | flops | bytes accessed | tf_op | source)
XLA Modules:
  0.0 34.6 jit_solution(3766309889131824233)
XLA Ops:
  0.0 0.0 copy-start
  0.0 33.1 %spectral_layer.1 = bf16[6,128,384]{2,1,0:T(8,128)(2,1)S(1)} custom-call(f32[6,128,384]{2,1,0:T(8,128)} %bitcast.13, f32[256,256,384]{2,1,0:T(8,128)} %fwd_hbm.1, f32[256,256,384]{2,1,0:T(8,128)} %inv_hbm.1, f32[256,256,128]{2,1,0:T(8,128)} %bitcast.12, bf16[512,768]{1,0:T(8,128)(2,1)} %constant.12.clone.dftf_hbm, bf16[512,768]{1,0:T(8,128)(2,1)} %constant.13.clone.dfti_hbm), custom_call_target="tpu_custom_call" | custom-call | tf_op jit(solution)/shard_map/spectral_layer/pallas_call | solution.py:235
  33.1 0.0 copy-done
  33.1 1.4 %fusion.8 = f32[1,128,6,384]{3,1,2,0:T(8,128)} fusion(f32[1,128,6,384]{3,1,2,0:T(8,128)S(1)} %copy-done, bf16[6,128,384]{2,1,0:T(8,128)(2,1)S(1)} %spectral_layer.1), kind=kLoop, calls=%fused_computation.9 | loop fusion | flops 2949120 | bytes 2949120 | tf_op jit(solution)/shard_map/add | solution.py:272
Async XLA Ops:
  0.0 33.1 %copy-start = (f32[1,128,6,384]{3,1,2,0:T(8,128)S(1)}, f32[1,128,6,384]{3,1,2,0:T(8,128)}, u32[]{:S(2)}) copy-start(f32[1,128,6,384]{3,1,2,0:T(8,128)} %param.6) | copy-start | bytes 3538948
where the time goes:
time: 34.7 us; the launch traced here: 34.6 us
  Pallas kernels  33.1 us (95%)
  other arithmetic  1.44 us (4%)
    pallas_call x1, Pallas kernels, local_layer(): pl.pallas_call(kernel, out_shape=jax.ShapeDtypeStruct((2 * TT, CH, JH), B...  33.1 us
    add x1, other arithmetic, local_layer(): return field_in + jax.nn.gelu(wave.astype(F32), approximate=True)  1.44 us

commit v1 on v0

--- a/solution.py
+++ b/solution.py
@@ -32,6 +32,7 @@
 
 
 ORDER = chip_order()
+COLOURED = sorted(ORDER + [(0, 0, 0)], key=lambda o: sum(o) % 2)
 
 
 def pair_of_device():
@@ -57,9 +58,9 @@
     return lax.dot_general(a, b, (((ca,), (cb,)), ((), ())), preferred_element_type=F32)
 
 
-def kernel(x_hbm, fwd_hbm, inv_hbm, mix_hbm, dftf_hbm, dfti_hbm, y_ref,
+def kernel(x_hbm, fwd_hbm, inv_hbm, mix_hbm, dftf_hbm, dfti_hbm, out_ref,
            xv, xb, xr, dftf, dfti, acc, sbuf, rbuf, tabf, tabi, tf, ti, wbuf, wt, gat, xm,
-           zf, bf, bfull, sbuf2, rbuf2, rbt, ysend, lsem, wsem, xsem, a1sem, a2sem, yesem):
+           zf, bf, bfull, sbuf2, rbuf2, rbt, ysend, yrecv, lsem, wsem, xsem, a1sem, a2sem, yesem):
     h = lax.axis_index("lon")
     p = lax.axis_index("lat")
     d = p * 2 + h
@@ -68,11 +69,14 @@
     def wrap(v):
         return jnp.where(v >= 4, v - 4, v)
     z, y, x = lax.div(p, 16), lax.rem(lax.div(p, 4), 4), lax.rem(p, 4)
-    zq = [wrap(z + i) * 16 for i in range(4)]
-    yq = [wrap(y + i) * 4 for i in range(4)]
+    step = lambda i: jnp.where(h == 0, i, (4 - i) % 4)
+    zq = [wrap(z + step(i)) * 16 for i in range(4)]
+    yq = [wrap(y + step(i)) * 4 for i in range(4)]
     xq = [wrap(x + i) for i in range(4)]
 
-    pair = 2 * (lax.rem(z + y + x, 2) * (CHIPS // 2) + lax.div(p, 2)) + h
+    colour = lax.rem(z + y + x, 2)
+    xc = [lax.rem(x + step(i) + colour, 4) for i in range(4)]
+    pair = 2 * (colour * (CHIPS // 2) + lax.div(p, 2)) + h
 
     loads = [
         pltpu.make_async_copy(x_hbm, xv, lsem.at[0]),
@@ -98,9 +102,9 @@
     for u in range(2):
         for t in range(TT):
             xb[u, pl.ds(t * CH, CH), :] = xv[u * TT + t].astype(BF)
+    loads[1].wait()
     for i in range(WSLOTS):
         wcopy(i, i).start()
-    loads[1].wait()
     own = pl.ds(pl.multiple_of(h * JH, JH), JH)
     oth = pl.ds(pl.multiple_of((1 - h) * JH, JH), JH)
     acc[...] = dot(dftf[:, own], xb[h], 1, 1)
@@ -145,11 +149,17 @@
     sbuf[...] = (acc[...] + dot(dftf[:, oth], xr[...], 1, 1)).astype(BF).reshape(DEV, 4, TT * CH)
 
     def exchange(src, dst, sem):
-        for a, b, c in ORDER:
-            q = zq[a] + yq[b] + xq[c]
-            for e in range(2):
-                pltpu.make_async_remote_copy(src.at[2 * q + e], dst.at[d], sem.at[0], sem.at[1],
-                                             device_id=(0, e, q), device_id_type=MESH).start()
+        for a, b, c in COLOURED:
+            q = zq[a] + yq[b] + xc[c]
+
+            def both():
+                for e in range(2):
+                    pltpu.make_async_remote_copy(src.at[2 * q + e], dst.at[d], sem.at[0], sem.at[1],
+                                                 device_id=(0, e, q), device_id_type=MESH).start()
+            if a or b:
+                both()
+            else:
+                pl.when(q != p)(both)
         pltpu.make_async_remote_copy(src.at[d + 1 - 2 * h], dst.at[d], sem.at[0], sem.at[1],
                                      device_id=mate, device_id_type=MESH).start()
         dst[d] = src[d]
@@ -209,14 +219,20 @@
     rbt[...] = rbuf2[...].reshape(2 * DEG, TT * CH).T
 
     ysend[...] = dot(rbt[...], dfti[:, oth], 1, 0).astype(BF).reshape(TT, CH, JH)
-    ycopy = [pltpu.make_async_remote_copy(ysend.at[t], y_ref.at[h * TT + t], yesem.at[t], yesem.at[TT + t],
+    ycopy = [pltpu.make_async_remote_copy(ysend.at[t], yrecv.at[t], yesem.at[t], yesem.at[TT + t],
                                           device_id=mate, device_id_type=MESH) for t in range(TT)]
     for c in ycopy:
         c.start()
     first.wait_send()
-    y_ref[pl.ds(h * TT, TT)] = dot(rbt[...], dfti[:, own], 1, 0).astype(BF).reshape(TT, CH, JH)
+
+    def finish(base, wave):
+        rows = pl.ds(base, TT)
+        out_ref[rows] = xv[rows] + jax.nn.gelu(wave.astype(F32), approximate=True)
+
+    finish(h * TT, dot(rbt[...], dfti[:, own], 1, 0).astype(BF).reshape(TT, CH, JH))
     for c in ycopy:
         c.wait_recv()
+    finish((1 - h) * TT, yrecv[...])
 
     for c in xcopy + ycopy:
         c.wait_send()
@@ -232,9 +248,9 @@
         mix = jnp.transpose(mix_weights, (0, 1, 3, 2)).reshape(DEG, 2 * CH, CH)
         hbm = pl.BlockSpec(memory_space=pltpu.HBM)
         dma2, dma6 = pltpu.SemaphoreType.DMA((2,)), pltpu.SemaphoreType.DMA((2 * TT,))
-        y = pl.pallas_call(
+        out = pl.pallas_call(
             kernel,
-            out_shape=jax.ShapeDtypeStruct((2 * TT, CH, JH), BF),
+            out_shape=jax.ShapeDtypeStruct((2 * TT, CH, JH), F32),
             in_specs=[hbm] * 6,
             out_specs=pl.BlockSpec(memory_space=pltpu.VMEM),
             scratch_shapes=[
@@ -261,6 +277,7 @@
                 pltpu.VMEM((DEV, 4, TT * CH), BF),
                 pltpu.VMEM((TT * CH, 2 * DEG), BF),
                 pltpu.VMEM((TT, CH, JH), BF),
+                pltpu.VMEM((TT, CH, JH), BF),
                 pltpu.SemaphoreType.DMA((5,)),
                 pltpu.SemaphoreType.DMA((WSLOTS,)),
                 dma6, dma2, dma2, dma6,
@@ -268,7 +285,6 @@
             compiler_params=pltpu.CompilerParams(collective_id=0, has_side_effects=True, vmem_limit_bytes=48 * 1024 * 1024),
             name="spectral_layer",
         )(*[pltpu.with_memory_space_constraint(v, pltpu.HBM) for v in (x, fwd_table, inv_table, mix, jnp.asarray(fwd_np), jnp.asarray(inv_np))])
-        wave = jnp.transpose(y, (1, 0, 2))[None]
-        return field_in + jax.nn.gelu(wave.astype(F32), approximate=True)
+        return jnp.transpose(out, (1, 0, 2))[None]
 
     return jax.shard_map(local_layer, mesh=mesh, in_specs=(grid_spec, P(), P(), P()), out_specs=grid_spec, check_vma=False)

time: 34.7 us -> 33.6 us (0.968)
  other arithmetic: 1.44 us -> 0 us
  local copies, waits for them, and re-layouts: 0.01 us -> 1.02 us
  Pallas kernels: 33.1 us -> 32.3 us
    add x1 -> x0, other arithmetic: 1.44 us -> none  [local_layer(): return field_in + jax.nn.gelu(wave.astype(F32), approximate=True)]
    unnamed x2 -> x1, local copies, waits for them, and re-layouts: 0.01 us -> 1.02 us
    pallas_call x1, Pallas kernels: 33.1 us -> 32.3 us  [local_layer(): pl.pallas_call(kernel, out_shape=jax.ShapeDtypeStruct((2 * TT, CH, JH), F...]
where the time goes in v1:
time: 33.6 us; the launch traced here: 33.3 us
  Pallas kernels  32.3 us (96%)
  local copies, waits for them, and re-layouts  1.02 us (3%)
    pallas_call x1, Pallas kernels, local_layer(): pl.pallas_call(kernel, out_shape=jax.ShapeDtypeStruct((2 * TT, CH, JH), F...  32.3 us
    unnamed x1, local copies, waits for them, and re-layouts  1.02 us

profile of v1, /device:TPU:1, one launch (start us, length us, event | category | flops | bytes accessed | tf_op | source)
XLA Modules:
  0.0 33.3 jit_solution(4603003560006853626)
XLA Ops:
  0.0 32.3 %spectral_layer.1 = f32[6,128,384]{2,1,0:T(8,128)S(1)} custom-call(f32[6,128,384]{2,1,0:T(8,128)} %bitcast.11, f32[256,256,384]{2,1,0:T(8,128)} %fwd_hbm.1, f32[256,256,384]{2,1,0:T(8,128)} %inv_hbm.1, f32[256,256,128]{2,1,0:T(8,128)} %bitcast.10, bf16[512,768]{1,0:T(8,128)(2,1)} %constant.4.clone.dftf_hbm, bf16[512,768]{1,0:T(8,128)(2,1)} %constant.5.clone.dfti_hbm), custom_call_target="tpu_custom_call" | custom-call | tf_op jit(solution)/shard_map/spectral_layer/pallas_call | solution.py:251
  32.3 1.0 %copy.8 = f32[1,128,6,384]{3,1,2,0:T(8,128)} copy(f32[1,128,6,384]{3,1,2,0:T(8,128)S(1)} %bitcast.9) | data formatting | bytes 2359296

commit v2 on v1

--- a/solution.py
+++ b/solution.py
@@ -20,7 +20,7 @@
 LAT = 384
 WCH = 8
 WSLOTS = 16
-EARLY = 3
+EARLY = 5
 BLOCKS = DEG // WCH
 GROUP = 64
 
@@ -76,6 +76,7 @@
 
     colour = lax.rem(z + y + x, 2)
     xc = [lax.rem(x + step(i) + colour, 4) for i in range(4)]
+    xplain = [wrap(x + step(i)) for i in range(4)]
     pair = 2 * (colour * (CHIPS // 2) + lax.div(p, 2)) + h
 
     loads = [
@@ -148,9 +149,9 @@
         xcopy[t].wait_recv()
     sbuf[...] = (acc[...] + dot(dftf[:, oth], xr[...], 1, 1)).astype(BF).reshape(DEV, 4, TT * CH)
 
-    def exchange(src, dst, sem):
-        for a, b, c in COLOURED:
-            q = zq[a] + yq[b] + xc[c]
+    def exchange(src, dst, sem, order, xs):
+        for a, b, c in order:
+            q = zq[a] + yq[b] + xs[c]
 
             def both():
                 for e in range(2):
@@ -166,7 +167,7 @@
         return pltpu.make_async_remote_copy(src.at[pl.ds(0, DEV - 1)], dst.at[pl.ds(0, DEV - 1)], sem.at[0], sem.at[1],
                                             device_id=mate, device_id_type=MESH)
 
-    first = exchange(sbuf, rbuf, a1sem)
+    first = exchange(sbuf, rbuf, a1sem, COLOURED, xc)
 
     prepare_blocks(EARLY, BLOCKS - WSLOTS, True)
     prepare_blocks(BLOCKS - WSLOTS, BLOCKS, False)
@@ -212,7 +213,7 @@
 
     for t in range(TT):
         sbuf2[:, :, t * CH:(t + 1) * CH] = gat[t].astype(BF).reshape(DEV, 4, CH)
-    second = exchange(sbuf2, rbuf2, a2sem)
+    second = exchange(sbuf2, rbuf2, a2sem, ORDER, xplain)
     loads[4].wait()
     second.wait_recv()
 

time: 33.6 us -> 34.2 us (1.018)
  Pallas kernels: 32.3 us -> 33.1 us
    pallas_call x1, Pallas kernels: 32.3 us -> 33.1 us  [local_layer(): pl.pallas_call(kernel, out_shape=jax.ShapeDtypeStruct((2 * TT, CH, JH), F...]
where the time goes in v2:
time: 34.2 us; the launch traced here: 34.1 us
  Pallas kernels  33.1 us (97%)
  local copies, waits for them, and re-layouts  1.02 us (3%)
    pallas_call x1, Pallas kernels, local_layer(): pl.pallas_call(kernel, out_shape=jax.ShapeDtypeStruct((2 * TT, CH, JH), F...  33.1 us
    unnamed x1, local copies, waits for them, and re-layouts  1.02 us

profile of v2, /device:TPU:1, one launch (start us, length us, event | category | flops | bytes accessed | tf_op | source)
XLA Modules:
  0.0 34.1 jit_solution(125321039403014769)
XLA Ops:
  0.0 33.1 %spectral_layer.1 = f32[6,128,384]{2,1,0:T(8,128)S(1)} custom-call(f32[6,128,384]{2,1,0:T(8,128)} %bitcast.11, f32[256,256,384]{2,1,0:T(8,128)} %fwd_hbm.1, f32[256,256,384]{2,1,0:T(8,128)} %inv_hbm.1, f32[256,256,128]{2,1,0:T(8,128)} %bitcast.10, bf16[512,768]{1,0:T(8,128)(2,1)} %constant.4.clone.dftf_hbm, bf16[512,768]{1,0:T(8,128)(2,1)} %constant.5.clone.dfti_hbm), custom_call_target="tpu_custom_call" | custom-call | tf_op jit(solution)/shard_map/spectral_layer/pallas_call | solution.py:252
  33.1 1.0 %copy.8 = f32[1,128,6,384]{3,1,2,0:T(8,128)} copy(f32[1,128,6,384]{3,1,2,0:T(8,128)S(1)} %bitcast.9) | data formatting | bytes 2359296
